TPU v7x, 32 devices: a whole 2x2x4 slice. The times are simulated.
32 devices in a mesh: ka: 8 (over y, x, core), ga: 4 (over z).
Axes of the slice: x: 2, y: 2, z: 4, core: 2. Of those that a mesh axis runs over, the one named last changes fastest.
Arguments:
- pair_densities: float32 [8192, 8192], P('ka', 'ga'), may hold values from -0.0625 to 0.0625
- energies: float32 [8192], P('ka'), may hold values from -2 to 2
- coulomb: float32 [8192], P('ga'), may hold values from 0.2 to 2
- start: float32 [8192, 128], P('ka'), may hold values from -6 to 6
Outputs:
- alphas: float32 [4, 128], replicated
- betas: float32 [4, 128], replicated
- lanczos_vector: float32 [8192, 128], P('ka')
All inputs are finite; a program needn't handle non-finite values.
Results may differ from a plain program's by a relative error of at most 0.00013.
Values sent between devices are 32-bit elements; how exact they have to be, the bound alone decides.
No kernel may reach another device: no remote copies, remote signals or barrier semaphores. Data moves between devices by JAX's collectives and lax.ppermute only.
A program may use at most 64 MiB of HBM per device.

v0:
```python
import jax
import jax.numpy as jnp
from jax import lax
from jax.sharding import PartitionSpec as P

ITERS = 4
EPSILON = 1e-06


def per_device(pair_densities, energies, coulomb, start):
    precise = lax.Precision.HIGHEST
    vector_count = start.shape[1]

    def project(full_vector, extra_rows):
        projected = jnp.dot(
            pair_densities.T, full_vector, precision=precise, preferred_element_type=jnp.float32
        )
        projected = jnp.concatenate([projected] + extra_rows, axis=0)
        return lax.psum(projected, "ka")

    start_sq = lax.psum(jnp.sum(start * start, axis=0), "ka")
    full_vector = start / jnp.sqrt(start_sq + EPSILON)
    vector = full_vector
    previous = jnp.zeros_like(vector)
    beta_now = jnp.zeros((vector_count,), jnp.float32)
    alpha_rows = []
    beta_rows = []
    remainder_full = full_vector
    remainder_own = vector
    for step in range(ITERS):
        energy_row = jnp.sum(energies[:, None] * remainder_full * remainder_full, axis=0)[None, :]
        if step == 0:
            summed = project(remainder_full, [energy_row])
            projected = summed[:-1]
            energy_sum = summed[-1]
            vector = remainder_own
        else:
            square_row = jnp.sum(remainder_full * remainder_full, axis=0)[None, :]
            summed = project(remainder_full, [square_row, energy_row])
            beta_full = jnp.sqrt(summed[-2] + EPSILON)
            projected = summed[:-2] / beta_full
            energy_sum = summed[-1] / (beta_full * beta_full)
            beta_new = beta_full
            beta_rows.append(beta_new)
            previous = vector
            vector = remainder_own / beta_new
            beta_now = beta_new
        weighted = coulomb[:, None] * projected
        curvature = jnp.sum(projected * weighted, axis=0)[None, :]
        partial_value = jnp.dot(
            pair_densities, weighted, precision=precise, preferred_element_type=jnp.float32
        )
        combine_partial_value = jnp.concatenate([partial_value, curvature], axis=0)
        combined = lax.psum(combine_partial_value, "ga")
        mixed = combined[:-1]
        alpha_now = energy_sum + combined[-1]
        image = energies[:, None] * vector + mixed
        remainder_own = image - alpha_now * vector - beta_now * previous
        alpha_rows.append(alpha_now)
        if step + 1 < ITERS:
            remainder_full = remainder_own
    last_sq = lax.psum(jnp.sum(remainder_own * remainder_own, axis=0), "ka")
    beta_new = jnp.sqrt(last_sq + EPSILON)
    beta_rows.append(beta_new)
    vector = remainder_own / beta_new
    alpha_table = jnp.stack(alpha_rows)
    beta_table = jnp.stack(beta_rows)
    full_vector = vector
    return (alpha_table, beta_table, full_vector)


def solution(mesh):
    placed = (P("ka", "ga"), P("ka"), P("ga"), P("ka", None))
    return jax.shard_map(
        per_device, mesh=mesh, in_specs=placed, out_specs=(P(), P(), P("ka", None)), check_vma=False
    )
```

profile of v0, /device:TPU:0, one launch (start us, length us, event | category | flops | bytes accessed | tf_op | source)
XLA Modules:
  0.0 530.7 jit_solution(17635808133581083179)
XLA Ops:
  9.7 15.2 %psum.70 = f32[128]{0:T(128)S(1)} all-reduce(f32[128]{0:T(128)S(1)} %multiply_reduce_fusion.4), channel_id=1, replica_groups=mesh['ka'=8,'ga'=4] {'ka'}, use_global_device_ids=true, to_apply=%region_1.0 | all-reduce | flops 128 | bytes 1024 | tf_op jit(solution)/shard_map/psum | solution.py:21
  25.2 7.1 %convolution_bitcast_fusion.3 = f32[2048,128]{0,1:T(8,128)S(1)} fusion(f32[1024,2048]{1,0:T(8,128)} %param.4, f32[1024,128]{0,1:T(8,128)S(1)} %copy.39, f32[128]{0:T(128)S(1)} %add_sqrt_fusion.1), kind=kOutput, calls=%fused_computation.3 | convolution fusion | flops 3221356544 | bytes 9961984 | tf_op jit(solution)/shard_map/dot_general | solution.py:15
  33.4 56.5 %all-reduce.9.cloned.1.call-done = f32[2049,128]{0,1:T(8,128)} async-done(((f32[2049,128]{0,1:T(8,128)}), f32[2049,128]{0,1:T(8,128)}) %all-reduce.9.cloned.1.call-update) | async-done | bytes 1049104 | tf_op jit(solution)/shard_map/psum | solution.py:19
  89.9 1.5 fusion.20
  91.5 11.1 %fusion.8 = f32[1024,128]{0,1:T(8,128)S(1)} fusion(f32[1024,2048]{1,0:T(8,128)} %param.4, f32[2049,128]{0,1:T(8,128)S(1)} %copy-done.3, f32[2048]{0:T(1024)S(1)} %copy-done.4), kind=kOutput, calls=%fused_computation.16 | convolution fusion | flops 3221487616 | bytes 9969664 | tf_op jit(solution)/shard_map/dot_general | solution.py:50
  103.6 39.1 %all-reduce.11.cloned.1.call-done = f32[1025,128]{0,1:T(8,128)} async-done(((f32[1025,128]{0,1:T(8,128)}), f32[1025,128]{0,1:T(8,128)}) %all-reduce.11.cloned.1.call-update) | async-done | bytes 524816 | tf_op jit(solution)/shard_map/psum | solution.py:54
  145.2 7.0 %convolution_bitcast_fusion.2 = f32[2048,128]{0,1:T(8,128)S(1)} fusion(f32[1024,128]{0,1:T(8,128)S(1)} %get-tuple-element.28, f32[1024,2048]{1,0:T(8,128)} %param.4), kind=kOutput, calls=%fused_computation.2 | convolution fusion | flops 3221225472 | bytes 9961472 | tf_op jit(solution)/shard_map/dot_general | solution.py:15
  153.7 56.4 %all-reduce.13.cloned.1.call-done = f32[2050,128]{0,1:T(8,128)} async-done(((f32[2050,128]{0,1:T(8,128)}), f32[2050,128]{0,1:T(8,128)}) %all-reduce.13.cloned.1.call-update) | async-done | bytes 1049616 | tf_op jit(solution)/shard_map/psum | solution.py:19
  211.2 1.5 fusion.21
  212.8 10.9 %fusion.11 = f32[1024,128]{0,1:T(8,128)S(1)} fusion(f32[1024,2048]{1,0:T(8,128)} %param.4, f32[2048]{0:T(1024)S(1)} %copy-done.4, f32[2050,128]{0,1:T(8,128)S(1)} %copy-done.1, f32[128]{0:T(128)S(1)} %get-tuple-element.32), kind=kOutput, calls=%fused_computation.17 | convolution fusion | flops 3221749760 | bytes 9970176 | tf_op jit(solution)/shard_map/dot_general | solution.py:50
  224.6 39.0 %all-reduce.15.cloned.1.call-done = f32[1025,128]{0,1:T(8,128)} async-done(((f32[1025,128]{0,1:T(8,128)}), f32[1025,128]{0,1:T(8,128)}) %all-reduce.15.cloned.1.call-update) | async-done | bytes 524816 | tf_op jit(solution)/shard_map/psum | solution.py:54
  264.7 1.4 fusion.28
  266.4 7.0 %convolution_bitcast_fusion.1 = f32[2048,128]{0,1:T(8,128)S(1)} fusion(f32[1024,128]{0,1:T(8,128)S(1)} %get-tuple-element.25, f32[1024,2048]{1,0:T(8,128)} %param.4), kind=kOutput, calls=%fused_computation.1 | convolution fusion | flops 3221225472 | bytes 9961472 | tf_op jit(solution)/shard_map/dot_general | solution.py:15
  274.7 56.6 %all-reduce.17.cloned.1.call-done = f32[2050,128]{0,1:T(8,128)} async-done(((f32[2050,128]{0,1:T(8,128)}), f32[2050,128]{0,1:T(8,128)}) %all-reduce.17.cloned.1.call-update) | async-done | bytes 1049616 | tf_op jit(solution)/shard_map/psum | solution.py:19
  332.4 1.5 fusion.22
  334.0 10.9 %fusion.14 = f32[1024,128]{0,1:T(8,128)S(1)} fusion(f32[1024,2048]{1,0:T(8,128)} %param.4, f32[2048]{0:T(1024)S(1)} %copy-done.4, f32[2050,128]{0,1:T(8,128)S(1)} %copy-done.2, f32[128]{0:T(128)S(1)} %get-tuple-element.34), kind=kOutput, calls=%fused_computation.18 | convolution fusion | flops 3221749760 | bytes 9970176 | tf_op jit(solution)/shard_map/dot_general | solution.py:50
  346.1 38.8 %all-reduce.19.cloned.1.call-done = f32[1025,128]{0,1:T(8,128)} async-done(((f32[1025,128]{0,1:T(8,128)}), f32[1025,128]{0,1:T(8,128)}) %all-reduce.19.cloned.1.call-update) | async-done | bytes 524816 | tf_op jit(solution)/shard_map/psum | solution.py:54
  385.9 1.4 fusion.29
  387.6 7.0 %convolution_bitcast_fusion = f32[2048,128]{0,1:T(8,128)S(1)} fusion(f32[1024,128]{0,1:T(8,128)S(1)} %get-tuple-element.22, f32[1024,2048]{1,0:T(8,128)} %param.4), kind=kOutput, calls=%fused_computation | convolution fusion | flops 3221225472 | bytes 9961472 | tf_op jit(solution)/shard_map/dot_general | solution.py:15
  395.9 56.6 %all-reduce.21.cloned.1.call-done = f32[2050,128]{0,1:T(8,128)} async-done(((f32[2050,128]{0,1:T(8,128)}), f32[2050,128]{0,1:T(8,128)}) %all-reduce.21.cloned.1.call-update) | async-done | bytes 1049616 | tf_op jit(solution)/shard_map/psum | solution.py:19
  453.6 1.5 fusion.23
  455.2 10.9 %fusion.17 = f32[1024,128]{0,1:T(8,128)S(1)} fusion(f32[1024,2048]{1,0:T(8,128)} %param.4, f32[2048]{0:T(1024)S(1)} %copy-done.4, f32[2050,128]{0,1:T(8,128)S(1)} %copy-done, f32[128]{0:T(128)S(1)} %get-tuple-element.36), kind=kOutput, calls=%fused_computation.19 | convolution fusion | flops 3221749760 | bytes 9970176 | tf_op jit(solution)/shard_map/dot_general | solution.py:50
  467.5 38.6 %all-reduce.23.cloned.1.call-done = f32[1025,128]{0,1:T(8,128)} async-done(((f32[1025,128]{0,1:T(8,128)}), f32[1025,128]{0,1:T(8,128)}) %all-reduce.23.cloned.1.call-update) | async-done | bytes 524816 | tf_op jit(solution)/shard_map/psum | solution.py:54
  508.5 13.0 %psum.79 = f32[128]{0:T(128)S(1)} all-reduce(f32[128]{0:T(128)S(1)} %get-tuple-element.18), channel_id=1, replica_groups=mesh['ka'=8,'ga'=4] {'ka'}, use_global_device_ids=true, to_apply=%region_22.0 | all-reduce | flops 128 | bytes 1024 | tf_op jit(solution)/shard_map/psum | solution.py:62
  (72 shorter events, 25.7 us)
Async XLA Ops:
  7.2 17.7 %copy-start.5 = (f32[1024]{0:T(1024)S(1)}, f32[1024]{0:T(1024)}, u32[]{:S(2)}) copy-start(f32[1024]{0:T(1024)} %param.5) | copy-start | bytes 12292
  7.2 82.7 %all-reduce.9.cloned.1.call-start = ((), (), s32[]{:S(2)}) async-start(), calls=%async_computation | async-start | bytes 2228224 | tf_op jit(solution)/shard_map/psum | solution.py:19
  33.4 56.6 %copy-start.4 = (f32[2048]{0:T(1024)S(1)}, f32[2048]{0:T(1024)}, u32[]{:S(2)}) copy-start(f32[2048]{0:T(1024)} %param.6) | copy-start | bytes 24580
  33.4 109.2 %all-reduce.11.cloned.1.call-start = ((), (), s32[]{:S(2)}) async-start(), calls=%async_computation.1 | async-start | bytes 1179648 | tf_op jit(solution)/shard_map/psum | solution.py:54
  89.9 1.6 copy-start.3
  103.5 106.6 %all-reduce.13.cloned.1.call-start = ((), (), s32[]{:S(2)}) async-start(), calls=%async_computation.2 | async-start | bytes 2228224 | tf_op jit(solution)/shard_map/psum | solution.py:19
  153.5 110.2 %all-reduce.15.cloned.1.call-start = ((), (), s32[]{:S(2)}) async-start(), calls=%async_computation.3 | async-start | bytes 1179648 | tf_op jit(solution)/shard_map/psum | solution.py:54
  210.1 2.7 copy-start.1
  224.6 106.7 %all-reduce.17.cloned.1.call-start = ((), (), s32[]{:S(2)}) async-start(), calls=%async_computation.4 | async-start | bytes 2228224 | tf_op jit(solution)/shard_map/psum | solution.py:19
  274.7 110.2 %all-reduce.19.cloned.1.call-start = ((), (), s32[]{:S(2)}) async-start(), calls=%async_computation.5 | async-start | bytes 1179648 | tf_op jit(solution)/shard_map/psum | solution.py:54
  331.3 2.7 copy-start.2
  345.8 106.7 %all-reduce.21.cloned.1.call-start = ((), (), s32[]{:S(2)}) async-start(), calls=%async_computation.6 | async-start | bytes 2228224 | tf_op jit(solution)/shard_map/psum | solution.py:19
  395.8 110.2 %all-reduce.23.cloned.1.call-start = ((), (), s32[]{:S(2)}) async-start(), calls=%async_computation.7 | async-start | bytes 1179648 | tf_op jit(solution)/shard_map/psum | solution.py:54
  452.5 2.7 copy-start
Sparse Core Ops, SparseCore 0:
  33.5 56.3 all-reduce.8
  103.7 38.9 all-reduce.10
  153.6 56.4 all-reduce.12
  224.7 38.9 all-reduce.14
  274.8 56.4 all-reduce.16
  345.9 38.9 all-reduce.18
  396.0 56.4 all-reduce.20
  467.1 38.9 all-reduce.22
where the time goes:
time: 531 us
  waiting for transfers between devices  382 us (72%)
  matrix products  71.9 us (14%)
  blocking collectives  28.1 us (5%)
  other arithmetic  26.1 us (5%)
  between operations  14.3 us (3%)
  local copies, waits for them, and re-layouts  7.71 us (1%)
    psum x4, waiting for transfers between devices, project(): return lax.psum(projected, 'ka')  226 us
    psum x4, waiting for transfers between devices, per_device(): combined = lax.psum(combine_partial_value, 'ga')  156 us
    dot_general x4, matrix products, per_device(): jnp.dot(pair_densities, weighted, precision=precise, preferred_element_ty...  43.8 us
    dot_general x4, matrix products, project(): jnp.dot(pair_densities.T, full_vector, precision=precise, preferred_eleme...  28.1 us
    psum x1, blocking collectives, per_device(): start_sq = lax.psum(jnp.sum(start * start, axis=0), 'ka')  15.2 us
    psum x1, blocking collectives, per_device(): last_sq = lax.psum(jnp.sum(remainder_own * remainder_own, axis=0), 'ka')  13 us
  transfers between devices with their start and end apart: 8, of which 8 were waited for; matrix products, arithmetic and copies ran while one was open for 0% of the time, Pallas kernels for 0%

commit v1 on v0

--- a/solution.py
+++ b/solution.py
@@ -51,7 +51,11 @@
             pair_densities, weighted, precision=precise, preferred_element_type=jnp.float32
         )
         combine_partial_value = jnp.concatenate([partial_value, curvature], axis=0)
-        combined = lax.psum(combine_partial_value, "ga")
+        combined = combine_partial_value
+        for hop in (1, 2):
+            combined = combined + lax.ppermute(
+                combined, "ga", [(dev, dev ^ hop) for dev in range(4)]
+            )
         mixed = combined[:-1]
         alpha_now = energy_sum + combined[-1]
         image = energies[:, None] * vector + mixed

time: 531 us -> 557 us (1.049); the launches traced: 531 us -> 549 us
  matrix products: 71.9 us -> 107 us
  waiting for transfers between devices: 382 us -> 361 us
  starting transfers between devices: 0.73 us -> 16 us
  other arithmetic: 26.1 us -> 17.2 us
    psum x4 -> x0, waiting for transfers between devices: 156 us -> none  [per_device(): combined = lax.psum(combine_partial_value, 'ga')]
    ppermute x0 -> x8, waiting for transfers between devices: none -> 134 us  [per_device(): lax.ppermute(combined, 'ga', [(dev, dev ^ hop) for dev in range(4)])]
    dot_general x4, matrix products: 28.1 us -> 68.2 us  [project(): jnp.dot(pair_densities.T, full_vector, precision=precise, preferred_eleme...]
    ppermute x0 -> x8, starting transfers between devices: none -> 15.8 us  [per_device(): lax.ppermute(combined, 'ga', [(dev, dev ^ hop) for dev in range(4)])]
  transfers between devices with their start and end apart: 8 -> 12, of which waited for: 8 -> 12; matrix products, arithmetic and copies ran while one was open for 0% -> 0% of each run, Pallas kernels for 0% -> 0%
where the time goes in v1:
time: 557 us; the launch traced here: 549 us
  waiting for transfers between devices  361 us (65%)
  matrix products  107 us (19%)
  blocking collectives  26.9 us (5%)
  other arithmetic  17.2 us (3%)
  starting transfers between devices  16 us (3%)
  between operations  14.2 us (3%)
  local copies, waits for them, and re-layouts  6.74 us (1%)
    psum x4, waiting for transfers between devices, project(): return lax.psum(projected, 'ka')  226 us
    ppermute x8, waiting for transfers between devices, per_device(): lax.ppermute(combined, 'ga', [(dev, dev ^ hop) for dev in range(4)])  134 us
    dot_general x4, matrix products, project(): jnp.dot(pair_densities.T, full_vector, precision=precise, preferred_eleme...  68.2 us
    dot_general x4, matrix products, per_device(): jnp.dot(pair_densities, weighted, precision=precise, preferred_element_ty...  39.2 us
    ppermute x8, starting transfers between devices, per_device(): lax.ppermute(combined, 'ga', [(dev, dev ^ hop) for dev in range(4)])  15.8 us
    psum x1, blocking collectives, per_device(): start_sq = lax.psum(jnp.sum(start * start, axis=0), 'ka')  15.1 us
    psum x1, blocking collectives, per_device(): last_sq = lax.psum(jnp.sum(remainder_own * remainder_own, axis=0), 'ka')  11.8 us
  transfers between devices with their start and end apart: 12, of which 12 were waited for; matrix products, arithmetic and copies ran while one was open for 0% of the time, Pallas kernels for 0%

profile of v1, /device:TPU:0, one launch (start us, length us, event | category | flops | bytes accessed | tf_op | source)
XLA Modules:
  0.0 549.2 jit_solution(14285285475619719911)
XLA Ops:
  8.5 15.1 %psum.42 = f32[128]{0:T(128)S(1)} all-reduce(f32[128]{0:T(128)S(1)} %multiply_reduce_fusion.4), channel_id=1, replica_groups=mesh['ka'=8,'ga'=4] {'ka'}, use_global_device_ids=true, to_apply=%region_1.0 | all-reduce | flops 128 | bytes 1024 | tf_op jit(solution)/shard_map/psum | solution.py:21
  24.9 15.6 %convolution_bitcast_fusion.3 = f32[2048,128]{1,0:T(8,128)S(1)} fusion(f32[1024,2048]{1,0:T(8,128)} %param.4, f32[1024,128]{1,0:T(8,128)S(1)} %copy-done, f32[128]{0:T(128)S(1)} %add_sqrt_fusion.1), kind=kOutput, calls=%fused_computation.3 | convolution fusion | flops 3221356544 | bytes 9961984 | tf_op jit(solution)/shard_map/dot_general | solution.py:15
  41.6 56.3 %all-reduce.5.cloned.1.call-done = f32[2049,128]{1,0:T(8,128)} async-done(((f32[2049,128]{1,0:T(8,128)}), f32[2049,128]{1,0:T(8,128)}) %all-reduce.5.cloned.1.call-update) | async-done | bytes 1049104 | tf_op jit(solution)/shard_map/psum | solution.py:19
  99.7 9.9 %fusion.8 = f32[1024,128]{1,0:T(8,128)S(1)} fusion(f32[1024,2048]{1,0:T(8,128)} %param.4, f32[2049,128]{1,0:T(8,128)} %all-reduce.5.cloned.1.call-done, f32[2048]{0:T(1024)S(1)} %copy-done.4), kind=kOutput, calls=%fused_computation.16 | convolution fusion | flops 3221487616 | bytes 9969664 | tf_op jit(solution)/shard_map/dot_general | solution.py:50
  111.1 11.6 %collective-permute-done = f32[1025,128]{1,0:T(8,128)S(1)} collective-permute-done((f32[1025,128]{1,0:T(8,128)S(1)}, f32[1025,128]{1,0:T(8,128)S(1)}, u32[]{:S(2)}, u32[]{:S(2)}) %collective-permute-start) | collective-permute-done | bytes 524832 | tf_op jit(solution)/shard_map/ppermute | solution.py:56
  122.8 2.5 collective-permute-start.1
  125.3 22.0 %collective-permute-done.1 = f32[1025,128]{1,0:T(8,128)S(1)} collective-permute-done((f32[1025,128]{1,0:T(8,128)S(1)}, f32[1025,128]{1,0:T(8,128)S(1)}, u32[]{:S(2)}, u32[]{:S(2)}) %collective-permute-start.1) | collective-permute-done | bytes 524832 | tf_op jit(solution)/shard_map/ppermute | solution.py:56
  148.3 25.7 %convolution_bitcast_fusion.2 = f32[2048,128]{1,0:T(8,128)S(1)} fusion(f32[1024,128]{1,0:T(8,128)S(1)} %get-tuple-element.22, f32[1024,2048]{1,0:T(8,128)S(1)} %bitcast.51), kind=kOutput, calls=%fused_computation.2 | convolution fusion | flops 3221225472 | bytes 9961472 | tf_op jit(solution)/shard_map/dot_general | solution.py:15
  176.3 56.6 %all-reduce.7.cloned.1.call-done = f32[2050,128]{1,0:T(8,128)} async-done(((f32[2050,128]{1,0:T(8,128)}), f32[2050,128]{1,0:T(8,128)}) %all-reduce.7.cloned.1.call-update) | async-done | bytes 1049616 | tf_op jit(solution)/shard_map/psum | solution.py:19
  235.4 10.1 %fusion.11 = f32[1024,128]{1,0:T(8,128)S(1)} fusion(f32[1024,2048]{1,0:T(8,128)} %param.4, f32[2048]{0:T(1024)S(1)} %copy-done.4, f32[2050,128]{1,0:T(8,128)S(1)} %copy-done.1, f32[128]{0:T(128)S(1)} %get-tuple-element.24), kind=kOutput, calls=%fused_computation.17 | convolution fusion | flops 3221749760 | bytes 9970176 | tf_op jit(solution)/shard_map/dot_general | solution.py:50
  247.0 11.6 %collective-permute-done.2 = f32[1025,128]{1,0:T(8,128)S(1)} collective-permute-done((f32[1025,128]{1,0:T(8,128)S(1)}, f32[1025,128]{1,0:T(8,128)S(1)}, u32[]{:S(2)}, u32[]{:S(2)}) %collective-permute-start.2) | collective-permute-done | bytes 524832 | tf_op jit(solution)/shard_map/ppermute | solution.py:56
  261.2 22.0 %collective-permute-done.3 = f32[1025,128]{1,0:T(8,128)S(1)} collective-permute-done((f32[1025,128]{1,0:T(8,128)S(1)}, f32[1025,128]{1,0:T(8,128)S(1)}, u32[]{:S(2)}, u32[]{:S(2)}) %collective-permute-start.3) | collective-permute-done | bytes 524832 | tf_op jit(solution)/shard_map/ppermute | solution.py:56
  283.6 13.6 %convolution_bitcast_fusion.1 = f32[2048,128]{1,0:T(8,128)S(1)} fusion(f32[1024,128]{1,0:T(8,128)S(1)} %get-tuple-element.21, f32[1024,2048]{1,0:T(8,128)S(1)} %bitcast.53), kind=kOutput, calls=%fused_computation.1 | convolution fusion | flops 3221225472 | bytes 9961472 | tf_op jit(solution)/shard_map/dot_general | solution.py:15
  299.5 56.6 %all-reduce.9.cloned.1.call-done = f32[2050,128]{1,0:T(8,128)} async-done(((f32[2050,128]{1,0:T(8,128)}), f32[2050,128]{1,0:T(8,128)}) %all-reduce.9.cloned.1.call-update) | async-done | bytes 1049616 | tf_op jit(solution)/shard_map/psum | solution.py:19
  358.6 10.1 %fusion.14 = f32[1024,128]{1,0:T(8,128)S(1)} fusion(f32[1024,2048]{1,0:T(8,128)} %param.4, f32[2048]{0:T(1024)S(1)} %copy-done.4, f32[2050,128]{1,0:T(8,128)S(1)} %copy-done.2, f32[128]{0:T(128)S(1)} %get-tuple-element.26), kind=kOutput, calls=%fused_computation.18 | convolution fusion | flops 3221749760 | bytes 9970176 | tf_op jit(solution)/shard_map/dot_general | solution.py:50
  370.2 11.6 %collective-permute-done.4 = f32[1025,128]{1,0:T(8,128)S(1)} collective-permute-done((f32[1025,128]{1,0:T(8,128)S(1)}, f32[1025,128]{1,0:T(8,128)S(1)}, u32[]{:S(2)}, u32[]{:S(2)}) %collective-permute-start.4) | collective-permute-done | bytes 524832 | tf_op jit(solution)/shard_map/ppermute | solution.py:56
  381.9 2.5 collective-permute-start.5
  384.4 22.0 %collective-permute-done.5 = f32[1025,128]{1,0:T(8,128)S(1)} collective-permute-done((f32[1025,128]{1,0:T(8,128)S(1)}, f32[1025,128]{1,0:T(8,128)S(1)}, u32[]{:S(2)}, u32[]{:S(2)}) %collective-permute-start.5) | collective-permute-done | bytes 524832 | tf_op jit(solution)/shard_map/ppermute | solution.py:56
  406.8 13.3 %convolution_bitcast_fusion = f32[2048,128]{1,0:T(8,128)S(1)} fusion(f32[1024,128]{1,0:T(8,128)S(1)} %get-tuple-element.20, f32[1024,2048]{1,0:T(8,128)S(1)} %bitcast.55), kind=kOutput, calls=%fused_computation | convolution fusion | flops 3221225472 | bytes 9961472 | tf_op jit(solution)/shard_map/dot_general | solution.py:15
  422.4 56.7 %all-reduce.11.cloned.1.call-done = f32[2050,128]{1,0:T(8,128)} async-done(((f32[2050,128]{1,0:T(8,128)}), f32[2050,128]{1,0:T(8,128)}) %all-reduce.11.cloned.1.call-update) | async-done | bytes 1049616 | tf_op jit(solution)/shard_map/psum | solution.py:19
  481.4 9.2 %fusion.17 = f32[1024,128]{1,0:T(8,128)S(1)} fusion(f32[1024,2048]{1,0:T(8,128)} %param.4, f32[2048]{0:T(1024)S(1)} %copy-done.4, f32[2050,128]{1,0:T(8,128)S(1)} %copy-done.3, f32[128]{0:T(128)S(1)} %get-tuple-element.28), kind=kOutput, calls=%fused_computation.19 | convolution fusion | flops 3221749760 | bytes 9970176 | tf_op jit(solution)/shard_map/dot_general | solution.py:50
  492.2 11.6 %collective-permute-done.6 = f32[1025,128]{1,0:T(8,128)S(1)} collective-permute-done((f32[1025,128]{1,0:T(8,128)S(1)}, f32[1025,128]{1,0:T(8,128)S(1)}, u32[]{:S(2)}, u32[]{:S(2)}) %collective-permute-start.6) | collective-permute-done | bytes 524832 | tf_op jit(solution)/shard_map/ppermute | solution.py:56
  506.3 22.0 %collective-permute-done.7 = f32[1025,128]{1,0:T(8,128)S(1)} collective-permute-done((f32[1025,128]{1,0:T(8,128)S(1)}, f32[1025,128]{1,0:T(8,128)S(1)}, u32[]{:S(2)}, u32[]{:S(2)}) %collective-permute-start.7) | collective-permute-done | bytes 524832 | tf_op jit(solution)/shard_map/ppermute | solution.py:56
  529.3 11.8 %psum.47 = f32[128]{0:T(128)S(1)} all-reduce(f32[128]{0:T(128)S(1)} %get-tuple-element.18), channel_id=1, replica_groups=mesh['ka'=8,'ga'=4] {'ka'}, use_global_device_ids=true, to_apply=%region_18.0 | all-reduce | flops 128 | bytes 1024 | tf_op jit(solution)/shard_map/psum | solution.py:66
  (79 shorter events, 35.1 us)
Async XLA Ops:
  7.2 17.7 %copy-start = (f32[1024,128]{1,0:T(8,128)S(1)}, f32[1024,128]{1,0:T(8,128)}, u32[]{:S(2)}) copy-start(f32[1024,128]{1,0:T(8,128)} %param.7) | copy-start | bytes 1572868
  7.2 90.8 %all-reduce.5.cloned.1.call-start = ((), (), s32[]{:S(2)}) async-start(), calls=%async_computation | async-start | bytes 2105344 | tf_op jit(solution)/shard_map/psum | solution.py:19
  41.6 56.4 %copy-start.4 = (f32[2048]{0:T(1024)S(1)}, f32[2048]{0:T(1024)}, u32[]{:S(2)}) copy-start(f32[2048]{0:T(1024)} %param.6) | copy-start | bytes 24580
  41.6 191.3 %all-reduce.7.cloned.1.call-start = ((), (), s32[]{:S(2)}) async-start(), calls=%async_computation.1 | async-start | bytes 2105344 | tf_op jit(solution)/shard_map/psum | solution.py:19
  98.0 50.3 %slice-start = ((s8[8388608]{0:T(1024)(128)(4,1)}), s8[4194304]{0:T(1024)(128)(4,1)S(1)}, s32[]{:S(2)}) async-start(s8[8388608]{0:T(1024)(128)(4,1)} %bitcast.50), calls=%async_computation.4 | async-start | bytes 8388608
  99.7 48.6 %slice-start.1 = ((s8[8388608]{0:T(1024)(128)(4,1)}), s8[4194304]{0:T(1024)(128)(4,1)S(1)}, s32[]{:S(2)}) async-start(s8[8388608]{0:T(1024)(128)(4,1)} %bitcast.50), calls=%async_computation.5 | async-start | bytes 8388608
  109.7 13.1 %collective-permute-start = (f32[1025,128]{1,0:T(8,128)S(1)}, f32[1025,128]{1,0:T(8,128)S(1)}, u32[]{:S(2)}, u32[]{:S(2)}) collective-permute-start(f32[1025,128]{1,0:T(8,128)S(1)} %pad_maximum_fusion.1), channel_id=1, source_target_pairs={{0,1},{1,0},{2,3},{3,2},{4,5},{5,4},{6,7},{7,6},{8,9},{9,8},{10,11... | collective-permute-start | bytes 1574408 | tf_op jit(solution)/shard_map/ppermute | solution.py:56
  122.8 25.2 %copy-start.5 = (f32[1024]{0:T(1024)S(1)}, f32[1024]{0:T(1024)}, u32[]{:S(2)}) copy-start(f32[1024]{0:T(1024)} %param.5) | copy-start | bytes 12292
  122.8 24.5 %collective-permute-start.1 = (f32[1025,128]{1,0:T(8,128)S(1)}, f32[1025,128]{1,0:T(8,128)S(1)}, u32[]{:S(2)}, u32[]{:S(2)}) collective-permute-start(f32[1025,128]{1,0:T(8,128)S(1)} %fusion.50), channel_id=1, source_target_pairs={{0,2},{1,3},{2,0},{3,1},{4,6},{5,7},{6,4},{7,5},{8,10},{9,11},{10,... | collective-permute-start | bytes 1574408 | tf_op jit(solution)/shard_map/ppermute | solution.py:56
  176.3 179.8 %all-reduce.9.cloned.1.call-start = ((), (), s32[]{:S(2)}) async-start(), calls=%async_computation.2 | async-start | bytes 2105344 | tf_op jit(solution)/shard_map/psum | solution.py:19
  232.9 2.5 copy-start.1
  233.7 49.9 %slice-start.2 = ((s8[8388608]{0:T(1024)(128)(4,1)}), s8[4194304]{0:T(1024)(128)(4,1)S(1)}, s32[]{:S(2)}) async-start(s8[8388608]{0:T(1024)(128)(4,1)} %bitcast.52), calls=%async_computation.6 | async-start | bytes 8388608
  235.4 48.2 %slice-start.3 = ((s8[8388608]{0:T(1024)(128)(4,1)}), s8[4194304]{0:T(1024)(128)(4,1)S(1)}, s32[]{:S(2)}) async-start(s8[8388608]{0:T(1024)(128)(4,1)} %bitcast.52), calls=%async_computation.7 | async-start | bytes 8388608
  245.6 13.1 %collective-permute-start.2 = (f32[1025,128]{1,0:T(8,128)S(1)}, f32[1025,128]{1,0:T(8,128)S(1)}, u32[]{:S(2)}, u32[]{:S(2)}) collective-permute-start(f32[1025,128]{1,0:T(8,128)S(1)} %pad_maximum_fusion.2), channel_id=1, source_target_pairs={{0,1},{1,0},{2,3},{3,2},{4,5},{5,4},{6,7},{7,6},{8,9},{9,8},{10,11... | collective-permute-start | bytes 1574408 | tf_op jit(solution)/shard_map/ppermute | solution.py:56
  258.7 24.5 %collective-permute-start.3 = (f32[1025,128]{1,0:T(8,128)S(1)}, f32[1025,128]{1,0:T(8,128)S(1)}, u32[]{:S(2)}, u32[]{:S(2)}) collective-permute-start(f32[1025,128]{1,0:T(8,128)S(1)} %fusion.49), channel_id=1, source_target_pairs={{0,2},{1,3},{2,0},{3,1},{4,6},{5,7},{6,4},{7,5},{8,10},{9,11},{10,... | collective-permute-start | bytes 1574408 | tf_op jit(solution)/shard_map/ppermute | solution.py:56
  299.5 179.6 %all-reduce.11.cloned.1.call-start = ((), (), s32[]{:S(2)}) async-start(), calls=%async_computation.3 | async-start | bytes 2105344 | tf_op jit(solution)/shard_map/psum | solution.py:19
  356.1 2.5 copy-start.2
  356.9 49.9 %slice-start.4 = ((s8[8388608]{0:T(1024)(128)(4,1)}), s8[4194304]{0:T(1024)(128)(4,1)S(1)}, s32[]{:S(2)}) async-start(s8[8388608]{0:T(1024)(128)(4,1)} %bitcast.54), calls=%async_computation.8 | async-start | bytes 8388608
  358.6 48.2 %slice-start.5 = ((s8[8388608]{0:T(1024)(128)(4,1)}), s8[4194304]{0:T(1024)(128)(4,1)S(1)}, s32[]{:S(2)}) async-start(s8[8388608]{0:T(1024)(128)(4,1)} %bitcast.54), calls=%async_computation.9 | async-start | bytes 8388608
  368.7 13.1 %collective-permute-start.4 = (f32[1025,128]{1,0:T(8,128)S(1)}, f32[1025,128]{1,0:T(8,128)S(1)}, u32[]{:S(2)}, u32[]{:S(2)}) collective-permute-start(f32[1025,128]{1,0:T(8,128)S(1)} %pad_maximum_fusion.3), channel_id=1, source_target_pairs={{0,1},{1,0},{2,3},{3,2},{4,5},{5,4},{6,7},{7,6},{8,9},{9,8},{10,11... | collective-permute-start | bytes 1574408 | tf_op jit(solution)/shard_map/ppermute | solution.py:56
  381.9 24.5 %collective-permute-start.5 = (f32[1025,128]{1,0:T(8,128)S(1)}, f32[1025,128]{1,0:T(8,128)S(1)}, u32[]{:S(2)}, u32[]{:S(2)}) collective-permute-start(f32[1025,128]{1,0:T(8,128)S(1)} %fusion.48), channel_id=1, source_target_pairs={{0,2},{1,3},{2,0},{3,1},{4,6},{5,7},{6,4},{7,5},{8,10},{9,11},{10,... | collective-permute-start | bytes 1574408 | tf_op jit(solution)/shard_map/ppermute | solution.py:56
  479.1 2.4 copy-start.3
  490.7 13.1 %collective-permute-start.6 = (f32[1025,128]{1,0:T(8,128)S(1)}, f32[1025,128]{1,0:T(8,128)S(1)}, u32[]{:S(2)}, u32[]{:S(2)}) collective-permute-start(f32[1025,128]{1,0:T(8,128)S(1)} %pad_maximum_fusion.4), channel_id=1, source_target_pairs={{0,1},{1,0},{2,3},{3,2},{4,5},{5,4},{6,7},{7,6},{8,9},{9,8},{10,11... | collective-permute-start | bytes 1574408 | tf_op jit(solution)/shard_map/ppermute | solution.py:56
  503.9 24.5 %collective-permute-start.7 = (f32[1025,128]{1,0:T(8,128)S(1)}, f32[1025,128]{1,0:T(8,128)S(1)}, u32[]{:S(2)}, u32[]{:S(2)}) collective-permute-start(f32[1025,128]{1,0:T(8,128)S(1)} %fusion.47), channel_id=1, source_target_pairs={{0,2},{1,3},{2,0},{3,1},{4,6},{5,7},{6,4},{7,5},{8,10},{9,11},{10,... | collective-permute-start | bytes 1574408 | tf_op jit(solution)/shard_map/ppermute | solution.py:56
Sparse Core Ops, SparseCore 0:
  41.7 56.2 all-reduce.4
  176.4 56.4 all-reduce.6
  299.6 56.4 all-reduce.8
  422.5 56.5 all-reduce.10
